TPU v7x, 32 devices: a 4x4x1 block of a 4x4x8 slice. The times are simulated.
32 devices in a mesh: dp: 1 (over z), tp: 32 (over y, x, core).
Axes of the slice: x: 4, y: 4, z: 1, core: 2. Of those that a mesh axis runs over, the one named last changes fastest.
The devices are a block of a 4x4x8 slice.
Arguments:
- x_a: bfloat16 [4096, 2048], P(('dp', 'tp'))
- x_b: bfloat16 [4096, 2048], P(('dp', 'tp'))
- labels_a: int32 [4096], P(('dp', 'tp'))
- labels_b: int32 [4096], P(('dp', 'tp'))
- w_head: bfloat16 [2048, 49152], P(None, 'tp')
Outputs:
- output 1: float32 [2], P('dp')
- output 2: bfloat16 [2048, 49152], P('dp', 'tp')
- output 3: bfloat16 [4096, 2048], P(('dp', 'tp'))
- output 4: bfloat16 [4096, 2048], P(('dp', 'tp'))
All inputs are finite; a program needn't handle non-finite values.
Results may differ from a plain program's by a relative error of at most 0.001.
Values are sent between devices in bfloat16 or wider.
A program may use at most 768 MiB of HBM per device.

v0:
```python
import functools
import math

import jax
import jax.numpy as jnp
from jax import lax
from jax.experimental import pallas as pl
from jax.experimental.pallas import tpu as pltpu
from jax.sharding import PartitionSpec as P

MESH = pl.DeviceIdType.MESH
F32 = jnp.float32
BF16 = jnp.bfloat16
RINGS = 4
BLOCKS = 4
HALF = 3
PIECES = 2 * HALF
MBLOCKS = 8
BUFS = 3


def head_kernel(group, *refs):
    chips = group // 2
    dma = pltpu.SemaphoreType.DMA
    regular = pltpu.SemaphoreType.REGULAR
    pl.run_scoped(
        functools.partial(head_body, group, *refs),
        x_sem=dma((2 * BLOCKS,)), w_sem=dma((1,)), wp_sem=dma((2,)), lab_sem=dma((2, chips)), sync=regular((3,)),
        ag_send=dma((4, BLOCKS * RINGS)), ag_recv=dma((chips, BLOCKS * RINGS)),
        e_sem=dma((PIECES,)), er_sem=dma((2,)), xt_sem=dma((1,)), xtr_sem=dma((2,)),
        st_send=dma((chips,)), st_recv=dma((chips,)), bc_send=dma((chips,)), bc_recv=dma((chips,)), ls_sem=dma((2,)),
        rs_send=dma((BUFS, BLOCKS, RINGS)), rs_recv=dma((BUFS, BLOCKS, RINGS)), credit=regular((BLOCKS, RINGS)),
        dw_send=dma((HALF,)), dw_recv=dma((2, HALF)), dw_credit=regular, dwo_sem=dma((HALF,)), dxo_sem=dma((BLOCKS, 2)))


def head_body(group, xa, xb, la, lb, w, loss, dw, dxa, dxb, e_hbm, xt_hbm,
              wv, xg, stage, stage1, xts, xtb, buf, dwb, m_run, s_run, t_run, labc,
              lab_in, st_out, st_in, bc_in, bc_out, ls_out, ls_in,
              x_sem, w_sem, wp_sem, lab_sem, sync, ag_send, ag_recv, e_sem, er_sem, xt_sem, xtr_sem, st_send, st_recv,
              bc_send, bc_recv, ls_sem, rs_send, rs_recv, credit, dw_send, dw_recv, dw_credit, dwo_sem, dxo_sem):
    chips = group // 2
    side = math.isqrt(chips)
    rows = xa.shape[0]
    slot_rows = 2 * rows
    rt = slot_rows // RINGS
    hb = xg.shape[2]
    pc = hb
    shard = w.shape[1]
    tokens = rows * group
    mb_rows = w.shape[0] // MBLOCKS
    lanes = lab_in.shape[2]

    me = lax.axis_index("tp")
    core = lax.rem(me, 2)
    chip = me // 2
    partner = me + 1 - 2 * core
    cx = lax.rem(chip, side)
    cy = chip // side
    diag = lax.rem(cx + cy, side)
    pos = (side * cy + diag, side * lax.rem(cx + 1, side) + diag)

    def dev(c):
        return {"tp": 2 * c + core}

    def chip_at(cycle, p):
        major, minor = p // side, lax.rem(p, side)
        if cycle == 0:
            yy = major
            xx = lax.rem(minor - major + side, side)
        else:
            xx = lax.rem(major + side - 1, side)
            yy = lax.rem(minor + 1 - major + side, side)
        return yy * side + xx

    def source(r, k):
        sign = -1 if r % 2 == 0 else 1
        return chip_at(r // 2, lax.rem(pos[r // 2] + sign * k + 2 * chips, chips))

    up = [source(r, 1) for r in range(RINGS)]
    down = [source(r, -1) for r in range(RINGS)]

    for b in range(BLOCKS):
        cols = pl.ds(b * hb, hb)
        pltpu.make_async_copy(xa.at[:, cols], xg.at[b, pl.ds(0, rows)], x_sem.at[2 * b]).start()
        pltpu.make_async_copy(xb.at[:, cols], xg.at[b, pl.ds(rows, rows)], x_sem.at[2 * b + 1]).start()
    pltpu.make_async_copy(w, wv.at[0], w_sem.at[0]).start()

    barrier = pltpu.get_barrier_semaphore()

    def is_near(c):
        near = c == up[0]
        for r in range(1, RINGS):
            near = near | (c == up[r])
        return near

    for r in range(RINGS):
        pl.semaphore_signal(barrier, inc=1, device_id=dev(up[r]), device_id_type=MESH)
    pl.semaphore_signal(barrier, inc=1, device_id={"tp": partner}, device_id_type=MESH)
    my_lab = lab_in.at[chip]
    my_lab[0:1, :] = la[...].astype(F32)
    my_lab[1:2, :] = lb[...].astype(F32)
    with jax.named_scope("barrier"):
        pl.semaphore_wait(barrier, RINGS + 1)

    def ag_copy(k, j, r):
        src = xg.at[j, pl.ds(pl.multiple_of(k * slot_rows + r * rt, rt), rt)]
        dst = xg.at[j, pl.ds(pl.multiple_of((k + 1) * slot_rows + r * rt, rt), rt)]
        return pltpu.make_async_remote_copy(
            src_ref=src, dst_ref=dst, send_sem=ag_send.at[lax.rem(k, 4), j * RINGS + r],
            recv_sem=ag_recv.at[k + 1, j * RINGS + r], device_id=dev(down[r]), device_id_type=MESH)

    for b in range(BLOCKS):
        cols = pl.ds(b * hb, hb)
        pltpu.make_async_copy(xa.at[:, cols], xg.at[b, pl.ds(0, rows)], x_sem.at[2 * b]).wait()
        pltpu.make_async_copy(xb.at[:, cols], xg.at[b, pl.ds(rows, rows)], x_sem.at[2 * b + 1]).wait()
        for r in range(RINGS):
            ag_copy(0, b, r).start()

    w_swap = pltpu.make_async_remote_copy(
        src_ref=w, dst_ref=wv.at[1], send_sem=wp_sem.at[0], recv_sem=wp_sem.at[1],
        device_id={"tp": partner}, device_id_type=MESH)
    w_swap.start()

    def lab_copy(d):
        return pltpu.make_async_remote_copy(
            src_ref=lab_in.at[chip], dst_ref=lab_in.at[chip], send_sem=lab_sem.at[0, d], recv_sem=lab_sem.at[1, d],
            device_id=dev(lax.rem(chip + d, chips)), device_id_type=MESH)

    def lab_start(near):
        def go(d, carry):
            is_to = is_near(lax.rem(chip + d, chips))

            @pl.when(is_to if near else jnp.logical_not(is_to))
            def _():
                lab_copy(d).start()
            return carry
        lax.fori_loop(1, chips, go, 0)

    def lab_wait(near):
        def go(d, carry):
            is_from = is_near(lax.rem(chip + chips - d, chips))

            @pl.when(is_from if near else jnp.logical_not(is_from))
            def _():
                lab_copy(d).wait_recv()
            return carry
        lax.fori_loop(1, chips, go, 0)

    def sync_signal(n):
        for r in range(RINGS):
            pl.semaphore_signal(sync.at[n], inc=1, device_id=dev(up[r]), device_id_type=MESH)

    def sync_wait(n):
        pl.semaphore_wait(sync.at[n], RINGS)

    lab_start(True)
    sync_signal(0)
    with jax.named_scope("w_wait"):
        pltpu.make_async_copy(w, wv.at[0], w_sem.at[0]).wait()

    sub_i = lax.broadcasted_iota(jnp.int32, (rt, 128), 0)
    lane_i = lax.broadcasted_iota(jnp.int32, (rt, 128), 1)
    eye = sub_i == lane_i
    row_lane = lax.broadcasted_iota(jnp.int32, (1, 128), 1)
    lab_sub = lax.broadcasted_iota(jnp.int32, (rt, lanes), 0)
    lab_lane = lax.broadcasted_iota(jnp.int32, (rt, lanes), 1)

    def to_row(col):
        return jnp.sum(jnp.where(eye, col, 0.0), axis=0, keepdims=True)

    def to_col(row):
        return jnp.sum(jnp.where(eye, row, 0.0), axis=1, keepdims=True)

    def fill_labels(lab, sources):
        for r in range(RINGS):
            row = lab_in[sources[r], r // 2:r // 2 + 1, :]
            col = jnp.sum(jnp.where(lab_lane == lab_sub + (r % 2) * rt, row, 0.0), axis=1, keepdims=True)
            lab[r * rt:(r + 1) * rt, :] = jnp.broadcast_to(col.astype(jnp.int32), (rt, 128))

    def sources_of(k):
        return [source(r, k) for r in range(RINGS)]

    def base(lp):
        owner = me if lp < HALF else partner
        return owner * shard + (lp % HALF) * pc

    chunk = slot_rows // 8
    lane_iota = lax.broadcasted_iota(jnp.int32, (chunk, 128), 1)
    cols4 = [slice(c * 128, (c + 1) * 128) for c in range(pc // 128)]
    shift = slice(pc, pc + 128)

    def z_dot(k0, lp):
        z = None
        for b in range(BLOCKS):
            part = jnp.dot(xg[b, pl.ds(k0, slot_rows), :],
                           wv[lp // HALF, b * hb:(b + 1) * hb, (lp % HALF) * pc:(lp % HALF + 1) * pc],
                           preferred_element_type=F32)
            z = part if z is None else z + part
        stage[lp, :, 0:pc] = z

    def z_stats(lp, lab):
        off = base(lp)
        for c in range(8):
            rs = slice(c * chunk, (c + 1) * chunk)
            z = [stage[lp, rs, cs] for cs in cols4]
            m = functools.reduce(jnp.maximum, z)
            e = [jnp.exp(v - m) for v in z]
            rel = lab[rs, :] - off
            t = functools.reduce(jnp.add, [jnp.where(lane_iota + i * 128 == rel, v, 0.0) for i, v in enumerate(z)])
            s = functools.reduce(jnp.add, e)
            for cs, v in zip(cols4, e):
                stage[lp, rs, cs] = v
            stage[lp, rs, shift] = m
            if lp == 0:
                m_run[rs, :] = m
                s_run[rs, :] = s
                t_run[rs, :] = t
            else:
                old = m_run[rs, :]
                new = jnp.maximum(old, m)
                m_run[rs, :] = new
                s_run[rs, :] = s_run[rs, :] * jnp.exp(old - new) + s * jnp.exp(m - new)
                t_run[rs, :] = t_run[rs, :] + t

    def e_write(slot, lp):
        return pltpu.make_async_copy(stage.at[lp], e_hbm.at[slot, lp], e_sem.at[lp])

    def xt_write(slot):
        return pltpu.make_async_copy(
            xts, xt_hbm.at[:, pl.ds(pl.multiple_of(slot * slot_rows, slot_rows), slot_rows)], xt_sem.at[0])

    def st_copy(slot, r):
        return pltpu.make_async_remote_copy(
            src_ref=st_out.at[slot, r], dst_ref=st_in.at[slot, r], send_sem=st_send.at[slot],
            recv_sem=st_recv.at[slot], device_id=dev(source(r, slot)), device_id_type=MESH)

    def poll(k, j):
        @pl.when(k < chips)
        def _():
            for r in range(RINGS):
                ag_copy(k - 1, j, r).wait_recv()

        @pl.when(k < chips - 1)
        def _():
            @pl.when(k >= 4)
            def _():
                for r in range(RINGS):
                    ag_copy(k - 4, j, r).wait_send()
            for r in range(RINGS):
                ag_copy(k, j, r).start()

    fill_labels(labc.at[0], [chip] * RINGS)

    def gather_step(k, carry):
        slot = k - 1
        k0 = pl.multiple_of(slot * slot_rows, slot_rows)
        lab = labc.at[lax.rem(slot, 2)]
        ahead = sources_of(lax.rem(slot + 1, chips))

        @pl.when(slot >= 1)
        def _():
            for lp in range(PIECES):
                e_write(slot - 1, lp).wait()
            xt_write(slot - 1).wait()

        with jax.named_scope("z0"):
            z_dot(k0, 0)
            z_dot(k0, 1)
            z_stats(0, lab)
        e_write(slot, 0).start()
        poll(k, 0)

        @pl.when(slot == 0)
        def _():
            sync_wait(0)
            sync_signal(1)
            w_swap.wait()

        with jax.named_scope("z1"):
            z_dot(k0, 2)
            z_dot(k0, 3)
            z_stats(1, lab)
            z_stats(2, lab)
        for lp in (1, 2):
            e_write(slot, lp).start()
        poll(k, 1)

        @pl.when(slot == 0)
        def _():
            sync_wait(1)
            sync_signal(2)
            lab_wait(True)

        @pl.when(slot == 1)
        def _():
            lab_wait(False)
        with jax.named_scope("z2"):
            z_dot(k0, 4)
            z_dot(k0, 5)
            z_stats(3, lab)
            z_stats(4, lab)
            fill_labels(labc.at[lax.rem(slot + 1, 2)], ahead)
            for b in range(BLOCKS):
                xts[b * hb:(b + 1) * hb, :] = xg[b, pl.ds(k0, slot_rows), :].T
        for lp in (3, 4):
            e_write(slot, lp).start()
        xt_write(slot).start()
        poll(k, 2)
        with jax.named_scope("z_end"):
            z_stats(5, lab)
        e_write(slot, 5).start()

        stats_scope = jax.named_scope("stats")
        stats_scope.__enter__()
        lane_m = m_run[...]
        m = jnp.max(lane_m, axis=1, keepdims=True)
        s = jnp.sum(s_run[...] * jnp.exp(lane_m - m), axis=1, keepdims=True)
        t = jnp.sum(t_run[...], axis=1, keepdims=True)
        for r in range(RINGS):
            rs = slice(r * rt, (r + 1) * rt)
            tile = st_out.at[slot, r]
            tile[0:1, :] = to_row(m[rs])
            tile[1:2, :] = to_row(s[rs])
            tile[2:3, :] = to_row(t[rs])
        stats_scope.__exit__(None, None, None)

        @pl.when(slot == 0)
        def _():
            for r in range(RINGS):
                st_in[0, r] = st_out[0, r]

        @pl.when(slot >= 1)
        def _():
            for r in range(RINGS):
                st_copy(slot, r).start()

        @pl.when(slot == 0)
        def _():
            sync_wait(2)
            lab_start(False)
        poll(k, 3)
        return carry

    lax.fori_loop(1, chips + 1, gather_step, 0)

    def e_read(slot, odd):
        return pltpu.make_async_copy(e_hbm.at[slot], stage1 if odd else stage, er_sem.at[odd])

    e_read(1, 1).start()
    for lp in range(PIECES):
        e_write(chips - 1, lp).wait()
    e_read(2, 0).start()
    xt_write(chips - 1).wait()

    def xt_read(mb):
        return pltpu.make_async_copy(
            xt_hbm.at[pl.ds(pl.multiple_of(mb * mb_rows, mb_rows), mb_rows), :], xtb.at[lax.rem(mb, 2)],
            xtr_sem.at[lax.rem(mb, 2)])

    xt_read(0).start()
    buf[0] = jnp.zeros(buf.shape[1:], F32)
    for k in range(chips - 5, chips - 1):
        for j in range(BLOCKS):
            for r in range(RINGS):
                ag_copy(k, j, r).wait_send()

    def st_wait(k, carry):
        pltpu.make_async_copy(st_in.at[k], st_in.at[k], st_recv.at[k]).wait()
        return carry

    with jax.named_scope("st_wait"):
        lax.fori_loop(1, chips, st_wait, 0)
    inside = row_lane < rt
    parts = []
    for r in range(RINGS):
        m = st_in[0, r, 0:1, :]
        for k in range(1, chips):
            m = jnp.maximum(m, st_in[k, r, 0:1, :])
        s = jnp.zeros_like(m)
        t = jnp.zeros_like(m)
        for k in range(chips):
            s = s + st_in[k, r, 1:2, :] * jnp.exp(st_in[k, r, 0:1, :] - m)
            t = t + st_in[k, r, 2:3, :]
        bc_out[r:r + 1, :] = m
        bc_out[RINGS + r:RINGS + r + 1, :] = s
        parts.append(jnp.sum(jnp.where(inside, m + jnp.log(s) - t, 0.0), axis=1, keepdims=True))
    for mb in range(2):
        both = jnp.broadcast_to(parts[2 * mb] + parts[2 * mb + 1], (1, 128))
        bc_out[mb:mb + 1, :] = jnp.where(inside, bc_out[mb:mb + 1, :], both)
    bc_in[chip] = bc_out[...]

    def bc_copy(d):
        return pltpu.make_async_remote_copy(
            src_ref=bc_out, dst_ref=bc_in.at[chip], send_sem=bc_send.at[d], recv_sem=bc_recv.at[d],
            device_id=dev(lax.rem(chip + d, chips)), device_id_type=MESH)

    def bc_start(d, carry):
        bc_copy(d).start()
        return carry

    def bc_wait_near(d, carry):
        @pl.when(is_near(lax.rem(chip + chips - d, chips)))
        def _():
            bc_copy(d).wait_recv()
        return carry

    def bc_wait_far(d, carry):
        @pl.when(jnp.logical_not(is_near(lax.rem(chip + chips - d, chips))))
        def _():
            bc_copy(d).wait_recv()
        bc_copy(d).wait_send()
        lab_copy(d).wait_send()
        pltpu.make_async_copy(st_out.at[d], st_out.at[d], st_send.at[d]).wait()
        return carry

    ls_copy = pltpu.make_async_remote_copy(
        src_ref=ls_out, dst_ref=ls_in, send_sem=ls_sem.at[0], recv_sem=ls_sem.at[1],
        device_id={"tp": partner}, device_id_type=MESH)

    lax.fori_loop(1, chips, bc_start, 0)
    with jax.named_scope("bc_near"):
        lax.fori_loop(1, chips, bc_wait_near, 0)

    def form_g(slot, src_stage):
        k0 = pl.multiple_of(slot * slot_rows, slot_rows)
        sources = sources_of(slot)
        lab = labc.at[0]
        fill_labels(lab, sources)
        for r in range(RINGS):
            rs = slice(r * rt, (r + 1) * rt)
            m_run[rs, :] = jnp.broadcast_to(to_col(bc_in[sources[r], r:r + 1, :]), (rt, 128))
            s_run[rs, :] = jnp.broadcast_to(
                1.0 / (to_col(bc_in[sources[r], RINGS + r:RINGS + r + 1, :]) * tokens), (rt, 128))
        for lp in range(PIECES):
            off = base(lp)
            for c in range(8):
                rs = slice(c * chunk, (c + 1) * chunk)
                rel = lab[rs, :] - off
                scale = jnp.exp(src_stage[lp, rs, shift] - m_run[rs, :]) * s_run[rs, :]
                for i, cs in enumerate(cols4):
                    g = src_stage[lp, rs, cs] * scale - jnp.where(lane_iota + i * 128 == rel, 1.0 / tokens, 0.0)
                    xg[lp, pl.ds(pl.multiple_of(k0 + c * chunk, chunk), chunk), cs] = g.astype(BF16)

    e_read(1, 1).wait()
    with jax.named_scope("g_first"):
        form_g(1, stage1)
    e_read(3, 1).start()

    def rs_copy(s, j, r):
        b0, b1 = lax.rem(s, BUFS), lax.rem(s + 1, BUFS)
        return pltpu.make_async_remote_copy(
            src_ref=buf.at[b0, j, pl.ds(r * rt, rt)], dst_ref=buf.at[b1, j, pl.ds(r * rt, rt)],
            send_sem=rs_send.at[b0, j, r], recv_sem=rs_recv.at[b1, j, r],
            device_id=dev(down[r]), device_id_type=MESH)

    def dw_copy(mb, o):
        return pltpu.make_async_remote_copy(
            src_ref=stage.at[o, :, pl.ds(0, pc)], dst_ref=stage1.at[lax.rem(mb, 2) * HALF + o, :, pl.ds(0, pc)], send_sem=dw_send.at[o],
            recv_sem=dw_recv.at[lax.rem(mb, 2), o], device_id={"tp": partner}, device_id_type=MESH)

    def dw_out(mb, o):
        return pltpu.make_async_copy(
            dwb.at[o], dw.at[pl.ds(pl.multiple_of(mb * mb_rows, mb_rows), mb_rows),
                             pl.ds(pl.multiple_of(o * pc, pc), pc)], dwo_sem.at[o])

    def dx_out(j):
        cols = pl.ds(pl.multiple_of(j * hb, hb), hb)
        return (pltpu.make_async_copy(xtb.at[0, pl.ds(0, rows), cols], dxa.at[:, cols], dxo_sem.at[j, 0]),
                pltpu.make_async_copy(xtb.at[0, pl.ds(rows, rows), cols], dxb.at[:, cols], dxo_sem.at[j, 1]))

    last = chips - 1
    g_iters = chips // 2
    dw_iters = MBLOCKS * PIECES
    dw_from = 1 + g_iters
    own_from = dw_from + dw_iters
    assert own_from == last * BLOCKS - BLOCKS + 1

    def dx_dot(slot, j):
        k0 = pl.multiple_of(slot * slot_rows, slot_rows)
        tile = None
        for lp in range(PIECES):
            part = lax.dot_general(
                xg[lp, pl.ds(k0, slot_rows), :],
                wv[lp // HALF, pl.ds(pl.multiple_of(j * hb, hb), hb), (lp % HALF) * pc:(lp % HALF + 1) * pc],
                (((1,), (1,)), ((), ())), preferred_element_type=F32)
            tile = part if tile is None else tile + part
        return tile

    def rs_arrive(s, j):
        with jax.named_scope("rs_wait"):
            for r in range(RINGS):
                rs_copy(s - 1, j, r).wait_recv()

    def rs_send_on(s, j):
        @pl.when(s >= 2)
        def _():
            for r in range(RINGS):
                pl.semaphore_wait(credit.at[j, r], 1)
        for r in range(RINGS):
            rs_copy(s, j, r).start()

    def rs_release(s, j):
        for r in range(RINGS):
            rs_copy(s - 1, j, r).wait_send()

        @pl.when(s - 1 <= last - 3)
        def _():
            for r in range(RINGS):
                pl.semaphore_signal(credit.at[j, r], inc=1, device_id=dev(up[r]), device_id_type=MESH)

    def scatter_g(i, carry):
        s = i // BLOCKS
        j = lax.rem(i, BLOCKS)
        b0 = lax.rem(s, BUFS)

        @pl.when(s >= 1)
        def _():
            rs_arrive(s, j)

        even = lax.rem(2 * i, chips)
        e_read(even, 0).wait()
        with jax.named_scope("dx_g"):
            buf[b0, j] = buf[b0, j] + dx_dot(s + 1, j)
            form_g(even, stage)
        rs_send_on(s, j)

        @pl.when(i < g_iters)
        def _():
            e_read(lax.rem(2 * i + 2, chips), 0).start()
            e_read(2 * i + 1, 1).wait()
            with jax.named_scope("g"):
                form_g(2 * i + 1, stage1)

        @pl.when(i < g_iters - 1)
        def _():
            e_read(2 * i + 3, 1).start()

        @pl.when(s >= 1)
        def _():
            rs_release(s, j)
        return carry

    with jax.named_scope("dx_first"):
        buf[0, 0] = dx_dot(1, 0)
    rs_send_on(0, 0)
    with jax.named_scope("bc_far"):
        lax.fori_loop(1, chips, bc_wait_far, 0)
    lax.fori_loop(1, 1 + g_iters, scatter_g, 0)
    pl.semaphore_signal(dw_credit, inc=1, device_id={"tp": partner}, device_id_type=MESH)
    total = bc_in[0]
    for c in range(1, chips):
        total = total + bc_in[c]
    ls_out[...] = total
    ls_copy.start()

    def scatter_dw(i, carry):
        s = i // BLOCKS
        j = lax.rem(i, BLOCKS)
        b0 = lax.rem(s, BUFS)
        q = i - dw_from
        mb = q // PIECES
        o = lax.rem(q, PIECES)
        rs_arrive(s, j)

        @pl.when(o == 0)
        def _():
            xt_read(mb).wait()

            @pl.when(mb < MBLOCKS - 1)
            def _():
                xt_read(mb + 1).start()

        @pl.when((o < HALF) & (mb >= 1))
        def _():
            dw_copy(mb - 1, o).wait_send()

        with jax.named_scope("dx_dw"):
            buf[b0, j] = buf[b0, j] + dx_dot(s + 1, j)
            stage[o, :, 0:pc] = jnp.dot(xtb[lax.rem(mb, 2)], xg[lax.rem(o + HALF, PIECES)], preferred_element_type=F32)
        rs_send_on(s, j)

        @pl.when((o == 0) & (mb != 1))
        def _():
            pl.semaphore_wait(dw_credit, 1)

        @pl.when(o < HALF)
        def _():
            dw_copy(mb, o).start()

        @pl.when(o >= HALF)
        def _():
            h = o - HALF
            dw_copy(mb, h).wait_recv()

            @pl.when(mb >= 1)
            def _():
                dw_out(mb - 1, h).wait()
            dwb[h] = (stage[o, :, 0:pc] + stage1[lax.rem(mb, 2) * HALF + h, :, 0:pc]).astype(BF16)
            dw_out(mb, h).start()

            @pl.when((h == HALF - 1) & (mb < MBLOCKS - 2))
            def _():
                pl.semaphore_signal(dw_credit, inc=1, device_id={"tp": partner}, device_id_type=MESH)

        rs_release(s, j)
        return carry

    lax.fori_loop(dw_from, own_from, scatter_dw, 0)

    def scatter_own(i, carry):
        s = i // BLOCKS
        j = lax.rem(i, BLOCKS)
        b0 = lax.rem(s, BUFS)
        rs_arrive(s, j)
        with jax.named_scope("dx"):
            buf[b0, j] = buf[b0, j] + dx_dot(s + 1, j)
        rs_send_on(s, j)

        with jax.named_scope("own"):
            stage1[j, :, 0:pc] = dx_dot(0, j)

        @pl.when(j == 1)
        def _():
            stage1[0, :, 0:pc] = dx_dot(0, 0)
        rs_release(s, j)
        return carry

    lax.fori_loop(own_from, last * BLOCKS, scatter_own, 0)

    def scatter_last(j, carry):
        rs_arrive(last, j)
        with jax.named_scope("out"):
            xtb[0, 0:slot_rows, pl.ds(pl.multiple_of(j * hb, hb), hb)] = (buf[last % BUFS, j] + stage1[j, :, 0:pc]).astype(BF16)
        for c in dx_out(j):
            c.start()
        rs_release(last, j)
        return carry

    lax.fori_loop(0, BLOCKS, scatter_last, 0)

    ls_copy.wait()
    both = (ls_out[...] + ls_in[...]) * (1.0 / tokens)
    loss[0] = both[0, lanes - 1]
    loss[1] = both[1, lanes - 1]
    for o in range(HALF):
        dw_copy(MBLOCKS - 1, o).wait_send()
        dw_out(MBLOCKS - 1, o).wait()
    for j in range(BLOCKS):
        for c in dx_out(j):
            c.wait()


def solution(mesh):
    group = mesh.shape["tp"]
    chips = group // 2

    def local_step(x_a, x_b, labels_a, labels_b, w_local):
        rows, hidden = x_a.shape
        shard = w_local.shape[1]
        slot_rows = 2 * rows
        all_rows = chips * slot_rows
        hb = hidden // BLOCKS
        pc = shard // HALF
        mb_rows = hidden // MBLOCKS
        any_spec = pl.BlockSpec(memory_space=pl.ANY)
        vmem_spec = pl.BlockSpec(memory_space=pltpu.VMEM)
        out = pl.pallas_call(
            functools.partial(head_kernel, group),
            name="head",
            out_shape=(
                jax.ShapeDtypeStruct((2,), F32),
                jax.ShapeDtypeStruct((hidden, shard), BF16),
                jax.ShapeDtypeStruct((rows, hidden), BF16),
                jax.ShapeDtypeStruct((rows, hidden), BF16),
                jax.ShapeDtypeStruct((chips, PIECES, slot_rows, pc + 128), F32),
                jax.ShapeDtypeStruct((hidden, all_rows), BF16),
            ),
            in_specs=[any_spec, any_spec, vmem_spec, vmem_spec, any_spec],
            out_specs=(pl.BlockSpec(memory_space=pltpu.SMEM), any_spec, any_spec, any_spec, any_spec, any_spec),
            scratch_shapes=[
                pltpu.VMEM((2, hidden, shard), BF16),
                pltpu.VMEM((PIECES, all_rows, pc), BF16),
                pltpu.VMEM((PIECES, slot_rows, pc + 128), F32),
                pltpu.VMEM((PIECES, slot_rows, pc + 128), F32),
                pltpu.VMEM((hidden, slot_rows), BF16),
                pltpu.VMEM((2, mb_rows, all_rows), BF16),
                pltpu.VMEM((BUFS, BLOCKS, slot_rows, hb), F32),
                pltpu.VMEM((HALF, mb_rows, pc), BF16),
                pltpu.VMEM((slot_rows, 128), F32),
                pltpu.VMEM((slot_rows, 128), F32),
                pltpu.VMEM((slot_rows, 128), F32),
                pltpu.VMEM((2, slot_rows, 128), jnp.int32),
                pltpu.VMEM((chips, 8, rows), F32),
                pltpu.VMEM((chips, RINGS, 8, 128), F32),
                pltpu.VMEM((chips, RINGS, 8, 128), F32),
                pltpu.VMEM((chips, 8, 128), F32),
                pltpu.VMEM((8, 128), F32),
                pltpu.VMEM((8, 128), F32),
                pltpu.VMEM((8, 128), F32),
            ],
            compiler_params=pltpu.CompilerParams(
                collective_id=0, has_side_effects=True, vmem_limit_bytes=67043328),
        )(x_a, x_b, labels_a.reshape(1, rows), labels_b.reshape(1, rows), w_local)
        return out[0], out[1], out[2], out[3]

    row_spec = P(("dp", "tp"), None)
    label_spec = P(("dp", "tp"))
    return jax.shard_map(local_step, mesh=mesh, in_specs=(row_spec, row_spec, label_spec, label_spec, P(None, "tp")), out_specs=(P("dp"), P("dp", "tp"), row_spec, row_spec), check_vma=False)
```

profile of v0, /device:TPU:97, one launch (start us, length us, event | category | flops | bytes accessed | tf_op | source)
XLA Modules:
  0.0 305.1 jit_solution(4213458943829086722)
XLA Ops:
  0.6 295.8 %head.1 = (f32[2]{0:T(128)}, bf16[2048,1536]{1,0:T(8,128)(2,1)}, bf16[128,2048]{1,0:T(8,128)(2,1)}, bf16[128,2048]{1,0:T(8,128)(2,1)}, f32[16,6,256,640]{3,2,1,0:T(8,128)}, /*index=5*/bf16[2048,4096]{1,0:T(8,128)(2,1)}) custom-call(bf16[128,2048]{1,0:T(8,128)(2,1)} %refs_0_.1, bf16[128,2048]{1,0:T(8,128)(2,1)} %refs_1_.1, s32[1,128]{1,0:T(1,128)} %bitcast.2, ...), custom_call_target="tpu_custom_call" | custom-call | tf_op jit(solution)/shard_map/head/pallas_call | solution.py:667
  296.4 1.1 copy.13
  297.5 0.0 copy-start.1
  297.5 0.0 copy-start
  297.5 6.0 %copy.14 = bf16[2048,1536]{1,0:T(8,128)(2,1)} copy(bf16[2048,1536]{1,0:T(8,128)(2,1)} %get-tuple-element.17) | data formatting | bytes 12582912
  303.5 0.0 copy-done.1
  303.5 0.8 copy.15
  304.3 0.0 copy-done
  304.3 0.8 copy.16
Async XLA Ops:
  297.5 6.0 %copy-start.1 = (bf16[128,2048]{1,0:T(8,128)(2,1)S(1)}, bf16[128,2048]{1,0:T(8,128)(2,1)}, u32[]{:S(2)}) copy-start(bf16[128,2048]{1,0:T(8,128)(2,1)} %get-tuple-element.18) | copy-start | bytes 1572868
  297.5 6.8 %copy-start = (bf16[128,2048]{1,0:T(8,128)(2,1)S(1)}, bf16[128,2048]{1,0:T(8,128)(2,1)}, u32[]{:S(2)}) copy-start(bf16[128,2048]{1,0:T(8,128)(2,1)} %get-tuple-element.19) | copy-start | bytes 1572868
where the time goes:
time: 305 us
  Pallas kernels  296 us (97%)
  local copies, waits for them, and re-layouts  8.69 us (3%)
    pallas_call x1, Pallas kernels, local_step(): pl.pallas_call(functools.partial(head_kernel, group), name='head', out_sh...  296 us
    unnamed x8, local copies, waits for them, and re-layouts  8.69 us

commit v1 on v0

--- a/solution.py
+++ b/solution.py
@@ -25,18 +25,19 @@
     regular = pltpu.SemaphoreType.REGULAR
     pl.run_scoped(
         functools.partial(head_body, group, *refs),
-        x_sem=dma((2 * BLOCKS,)), w_sem=dma((1,)), wp_sem=dma((2,)), lab_sem=dma((2, chips)), sync=regular((3,)),
+        x_sem=dma((2 * BLOCKS,)), w_sem=dma((HALF,)), wp_sem=dma((2, HALF)), lab_sem=dma((2, chips)), sync=regular((3,)),
         ag_send=dma((4, BLOCKS * RINGS)), ag_recv=dma((chips, BLOCKS * RINGS)),
-        e_sem=dma((PIECES,)), er_sem=dma((2,)), xt_sem=dma((1,)), xtr_sem=dma((2,)),
-        st_send=dma((chips,)), st_recv=dma((chips,)), bc_send=dma((chips,)), bc_recv=dma((chips,)), ls_sem=dma((2,)),
-        rs_send=dma((BUFS, BLOCKS, RINGS)), rs_recv=dma((BUFS, BLOCKS, RINGS)), credit=regular((BLOCKS, RINGS)),
-        dw_send=dma((HALF,)), dw_recv=dma((2, HALF)), dw_credit=regular, dwo_sem=dma((HALF,)), dxo_sem=dma((BLOCKS, 2)))
+        e_sem=dma((HALF,)), er_sem=dma((2,)), xt_sem=dma((MBLOCKS,)), xtr_sem=dma((2,)),
+        run_send=dma((chips, RINGS)), run_recv=dma((chips, RINGS)), bc_send=dma((chips,)), bc_recv=dma((chips,)),
+        ls_sem=dma((2,)), rs_send=dma((BUFS, BLOCKS, RINGS)), rs_recv=dma((BUFS, BLOCKS, RINGS)),
+        credit=regular((BLOCKS, RINGS)), dw_send=dma((HALF,)), dw_recv=dma((2, HALF)), dw_credit=regular,
+        dwo_sem=dma((HALF,)), dxo_sem=dma((BLOCKS, 2)))
 
 
 def head_body(group, xa, xb, la, lb, w, loss, dw, dxa, dxb, e_hbm, xt_hbm,
-              wv, xg, stage, stage1, xts, xtb, buf, dwb, m_run, s_run, t_run, labc,
-              lab_in, st_out, st_in, bc_in, bc_out, ls_out, ls_in,
-              x_sem, w_sem, wp_sem, lab_sem, sync, ag_send, ag_recv, e_sem, er_sem, xt_sem, xtr_sem, st_send, st_recv,
+              wv, xg, stage, xtb, buf, dwb, m_run, s_run, t_run, labc,
+              lab_in, run_out, run_in, bc_in, bc_out, ls_out, ls_in,
+              x_sem, w_sem, wp_sem, lab_sem, sync, ag_send, ag_recv, e_sem, er_sem, xt_sem, xtr_sem, run_send, run_recv,
               bc_send, bc_recv, ls_sem, rs_send, rs_recv, credit, dw_send, dw_recv, dw_credit, dwo_sem, dxo_sem):
     chips = group // 2
     side = math.isqrt(chips)
@@ -83,7 +84,17 @@
         cols = pl.ds(b * hb, hb)
         pltpu.make_async_copy(xa.at[:, cols], xg.at[b, pl.ds(0, rows)], x_sem.at[2 * b]).start()
         pltpu.make_async_copy(xb.at[:, cols], xg.at[b, pl.ds(rows, rows)], x_sem.at[2 * b + 1]).start()
-    pltpu.make_async_copy(w, wv.at[0], w_sem.at[0]).start()
+
+    def w_load(h):
+        return pltpu.make_async_copy(w.at[:, pl.ds(h * pc, pc)], wv.at[h], w_sem.at[h])
+
+    def w_swap(h):
+        return pltpu.make_async_remote_copy(
+            src_ref=w.at[:, pl.ds(h * pc, pc)], dst_ref=wv.at[HALF + h], send_sem=wp_sem.at[0, h],
+            recv_sem=wp_sem.at[1, h], device_id={"tp": partner}, device_id_type=MESH)
+
+    for h in range(HALF):
+        w_load(h).start()
 
     barrier = pltpu.get_barrier_semaphore()
 
@@ -99,6 +110,7 @@
     my_lab = lab_in.at[chip]
     my_lab[0:1, :] = la[...].astype(F32)
     my_lab[1:2, :] = lb[...].astype(F32)
+    buf[0] = jnp.zeros(buf.shape[1:], F32)
     with jax.named_scope("barrier"):
         pl.semaphore_wait(barrier, RINGS + 1)
 
@@ -116,10 +128,8 @@
         for r in range(RINGS):
             ag_copy(0, b, r).start()
 
-    w_swap = pltpu.make_async_remote_copy(
-        src_ref=w, dst_ref=wv.at[1], send_sem=wp_sem.at[0], recv_sem=wp_sem.at[1],
-        device_id={"tp": partner}, device_id_type=MESH)
-    w_swap.start()
+    for h in range(HALF):
+        w_swap(h).start()
 
     def lab_copy(d):
         return pltpu.make_async_remote_copy(
@@ -155,8 +165,8 @@
 
     lab_start(True)
     sync_signal(0)
-    with jax.named_scope("w_wait"):
-        pltpu.make_async_copy(w, wv.at[0], w_sem.at[0]).wait()
+    for h in range(HALF):
+        w_load(h).wait()
 
     sub_i = lax.broadcasted_iota(jnp.int32, (rt, 128), 0)
     lane_i = lax.broadcasted_iota(jnp.int32, (rt, 128), 1)
@@ -192,25 +202,23 @@
     def z_dot(k0, lp):
         z = None
         for b in range(BLOCKS):
-            part = jnp.dot(xg[b, pl.ds(k0, slot_rows), :],
-                           wv[lp // HALF, b * hb:(b + 1) * hb, (lp % HALF) * pc:(lp % HALF + 1) * pc],
-                           preferred_element_type=F32)
+            part = jnp.dot(xg[b, pl.ds(k0, slot_rows), :], wv[lp, b * hb:(b + 1) * hb, :], preferred_element_type=F32)
             z = part if z is None else z + part
-        stage[lp, :, 0:pc] = z
+        stage[0, lp, :, 0:pc] = z
 
     def z_stats(lp, lab):
         off = base(lp)
         for c in range(8):
             rs = slice(c * chunk, (c + 1) * chunk)
-            z = [stage[lp, rs, cs] for cs in cols4]
+            z = [stage[0, lp, rs, cs] for cs in cols4]
             m = functools.reduce(jnp.maximum, z)
             e = [jnp.exp(v - m) for v in z]
             rel = lab[rs, :] - off
             t = functools.reduce(jnp.add, [jnp.where(lane_iota + i * 128 == rel, v, 0.0) for i, v in enumerate(z)])
             s = functools.reduce(jnp.add, e)
             for cs, v in zip(cols4, e):
-                stage[lp, rs, cs] = v
-            stage[lp, rs, shift] = m
+                stage[0, lp, rs, cs] = v
+            stage[0, lp, rs, shift] = m
             if lp == 0:
                 m_run[rs, :] = m
                 s_run[rs, :] = s
@@ -222,19 +230,43 @@
                 s_run[rs, :] = s_run[rs, :] * jnp.exp(old - new) + s * jnp.exp(m - new)
                 t_run[rs, :] = t_run[rs, :] + t
 
-    def e_write(slot, lp):
-        return pltpu.make_async_copy(stage.at[lp], e_hbm.at[slot, lp], e_sem.at[lp])
-
-    def xt_write(slot):
+    def e_write(slot, pair):
+        two = pl.ds(2 * pair, 2)
+        return pltpu.make_async_copy(stage.at[0, two], e_hbm.at[slot, two], e_sem.at[pair])
+
+    def xt_write(slot, mb):
         return pltpu.make_async_copy(
-            xts, xt_hbm.at[:, pl.ds(pl.multiple_of(slot * slot_rows, slot_rows), slot_rows)], xt_sem.at[0])
-
-    def st_copy(slot, r):
+            xtb.at[1, :, pl.ds(mb * mb_rows, slot_rows)],
+            xt_hbm.at[pl.ds(mb * mb_rows, mb_rows), pl.ds(pl.multiple_of(slot * slot_rows, slot_rows), slot_rows)],
+            xt_sem.at[mb])
+
+    def run_copy(slot, r):
         return pltpu.make_async_remote_copy(
-            src_ref=st_out.at[slot, r], dst_ref=st_in.at[slot, r], send_sem=st_send.at[slot],
-            recv_sem=st_recv.at[slot], device_id=dev(source(r, slot)), device_id_type=MESH)
+            src_ref=run_out.at[slot, r], dst_ref=run_in.at[slot + 1, r], send_sem=run_send.at[slot, r],
+            recv_sem=run_recv.at[slot + 1, r], device_id=dev(down[r]), device_id_type=MESH)
+
+    def join_stats(slot):
+        with jax.named_scope("stats"):
+            lane_m = m_run[...]
+            m = jnp.max(lane_m, axis=1, keepdims=True)
+            s = jnp.sum(s_run[...] * jnp.exp(lane_m - m), axis=1, keepdims=True)
+            t = jnp.sum(t_run[...], axis=1, keepdims=True)
+            rows_mst = [[to_row(v[r * rt:(r + 1) * rt]) for v in (m, s, t)] for r in range(RINGS)]
+
+        @pl.when(slot >= 1)
+        def _():
+            for r in range(RINGS):
+                run_copy(slot - 1, r).wait_recv()
+        for r in range(RINGS):
+            m_r, s_r, t_r = rows_mst[r]
+            m_in = run_in[slot, r, 0:1, :]
+            m_new = jnp.maximum(m_in, m_r)
+            run_out[slot, r, 0:1, :] = m_new
+            run_out[slot, r, 1:2, :] = s_r * jnp.exp(m_r - m_new) + run_in[slot, r, 1:2, :] * jnp.exp(m_in - m_new)
+            run_out[slot, r, 2:3, :] = t_r + run_in[slot, r, 2:3, :]
 
     def poll(k, j):
+      with jax.named_scope("poll"):
         @pl.when(k < chips)
         def _():
             for r in range(RINGS):
@@ -250,137 +282,109 @@
                 ag_copy(k, j, r).start()
 
     fill_labels(labc.at[0], [chip] * RINGS)
+    for r in range(RINGS):
+        run_in[0, r, 0:1, :] = jnp.full((1, 128), -jnp.inf, F32)
+        run_in[0, r, 1:3, :] = jnp.zeros((2, 128), F32)
 
     def gather_step(k, carry):
         slot = k - 1
         k0 = pl.multiple_of(slot * slot_rows, slot_rows)
-        lab = labc.at[lax.rem(slot, 2)]
+        here = labc.at[lax.rem(slot, 2)]
+        other = labc.at[lax.rem(slot + 1, 2)]
         ahead = sources_of(lax.rem(slot + 1, chips))
 
         @pl.when(slot >= 1)
         def _():
-            for lp in range(PIECES):
-                e_write(slot - 1, lp).wait()
-            xt_write(slot - 1).wait()
-
-        with jax.named_scope("z0"):
+            e_write(slot - 1, 0).wait()
+
+        with jax.named_scope("u0"):
             z_dot(k0, 0)
             z_dot(k0, 1)
-            z_stats(0, lab)
-        e_write(slot, 0).start()
-        poll(k, 0)
+            z_stats(4, other)
+            z_stats(5, other)
+
+        @pl.when(slot == 0)
+        def _():
+            poll(k, 0)
+        poll(k, 1)
+
+        @pl.when(slot >= 1)
+        def _():
+            e_write(slot - 1, 2).start()
+            join_stats(slot - 1)
+            for r in range(RINGS):
+                run_copy(slot - 1, r).start()
+            e_write(slot - 1, 1).wait()
 
         @pl.when(slot == 0)
         def _():
             sync_wait(0)
             sync_signal(1)
-            w_swap.wait()
-
-        with jax.named_scope("z1"):
+            w_swap(0).wait()
+
+        with jax.named_scope("u1"):
             z_dot(k0, 2)
             z_dot(k0, 3)
-            z_stats(1, lab)
-            z_stats(2, lab)
-        for lp in (1, 2):
-            e_write(slot, lp).start()
-        poll(k, 1)
+            z_stats(0, here)
+            z_stats(1, here)
+        e_write(slot, 0).start()
+        poll(k, 2)
 
         @pl.when(slot == 0)
         def _():
             sync_wait(1)
             sync_signal(2)
             lab_wait(True)
+            poll(k, 3)
+            poll(k + 1, 0)
+            w_swap(1).wait()
+            w_swap(2).wait()
+
+        @pl.when(slot >= 1)
+        def _():
+            e_write(slot - 1, 2).wait()
+            for mb in range(MBLOCKS):
+                xt_write(slot - 1, mb).wait()
 
         @pl.when(slot == 1)
         def _():
             lab_wait(False)
-        with jax.named_scope("z2"):
+
+        with jax.named_scope("u2"):
             z_dot(k0, 4)
             z_dot(k0, 5)
-            z_stats(3, lab)
-            z_stats(4, lab)
-            fill_labels(labc.at[lax.rem(slot + 1, 2)], ahead)
-            for b in range(BLOCKS):
-                xts[b * hb:(b + 1) * hb, :] = xg[b, pl.ds(k0, slot_rows), :].T
-        for lp in (3, 4):
-            e_write(slot, lp).start()
-        xt_write(slot).start()
-        poll(k, 2)
-        with jax.named_scope("z_end"):
-            z_stats(5, lab)
-        e_write(slot, 5).start()
-
-        stats_scope = jax.named_scope("stats")
-        stats_scope.__enter__()
-        lane_m = m_run[...]
-        m = jnp.max(lane_m, axis=1, keepdims=True)
-        s = jnp.sum(s_run[...] * jnp.exp(lane_m - m), axis=1, keepdims=True)
-        t = jnp.sum(t_run[...], axis=1, keepdims=True)
-        for r in range(RINGS):
-            rs = slice(r * rt, (r + 1) * rt)
-            tile = st_out.at[slot, r]
-            tile[0:1, :] = to_row(m[rs])
-            tile[1:2, :] = to_row(s[rs])
-            tile[2:3, :] = to_row(t[rs])
-        stats_scope.__exit__(None, None, None)
-
-        @pl.when(slot == 0)
-        def _():
-            for r in range(RINGS):
-                st_in[0, r] = st_out[0, r]
+            z_stats(2, here)
+            z_stats(3, here)
+            fill_labels(other, ahead)
+            for mb in range(MBLOCKS):
+                at = mb * mb_rows % hb
+                xtb[1, :, mb * mb_rows:(mb + 1) * mb_rows] = xg[mb * mb_rows // hb, pl.ds(k0, slot_rows), at:at + mb_rows].T
+        e_write(slot, 1).start()
+        for mb in range(MBLOCKS):
+            xt_write(slot, mb).start()
 
         @pl.when(slot >= 1)
         def _():
-            for r in range(RINGS):
-                st_copy(slot, r).start()
+            poll(k, 3)
+            poll(k + 1, 0)
 
         @pl.when(slot == 0)
         def _():
             sync_wait(2)
             lab_start(False)
-        poll(k, 3)
         return carry
 
     lax.fori_loop(1, chips + 1, gather_step, 0)
-
-    def e_read(slot, odd):
-        return pltpu.make_async_copy(e_hbm.at[slot], stage1 if odd else stage, er_sem.at[odd])
-
-    e_read(1, 1).start()
-    for lp in range(PIECES):
-        e_write(chips - 1, lp).wait()
-    e_read(2, 0).start()
-    xt_write(chips - 1).wait()
-
-    def xt_read(mb):
-        return pltpu.make_async_copy(
-            xt_hbm.at[pl.ds(pl.multiple_of(mb * mb_rows, mb_rows), mb_rows), :], xtb.at[lax.rem(mb, 2)],
-            xtr_sem.at[lax.rem(mb, 2)])
-
-    xt_read(0).start()
-    buf[0] = jnp.zeros(buf.shape[1:], F32)
-    for k in range(chips - 5, chips - 1):
-        for j in range(BLOCKS):
-            for r in range(RINGS):
-                ag_copy(k, j, r).wait_send()
-
-    def st_wait(k, carry):
-        pltpu.make_async_copy(st_in.at[k], st_in.at[k], st_recv.at[k]).wait()
-        return carry
-
-    with jax.named_scope("st_wait"):
-        lax.fori_loop(1, chips, st_wait, 0)
+    with jax.named_scope("flush"):
+        z_stats(4, labc.at[(chips - 1) % 2])
+        z_stats(5, labc.at[(chips - 1) % 2])
+    e_write(chips - 1, 2).start()
+    join_stats(chips - 1)
+
     inside = row_lane < rt
     parts = []
     for r in range(RINGS):
-        m = st_in[0, r, 0:1, :]
-        for k in range(1, chips):
-            m = jnp.maximum(m, st_in[k, r, 0:1, :])
-        s = jnp.zeros_like(m)
-        t = jnp.zeros_like(m)
-        for k in range(chips):
-            s = s + st_in[k, r, 1:2, :] * jnp.exp(st_in[k, r, 0:1, :] - m)
-            t = t + st_in[k, r, 2:3, :]
+        m, s, t = (run_out[chips - 1, r, i:i + 1, :] for i in range(3))
         bc_out[r:r + 1, :] = m
         bc_out[RINGS + r:RINGS + r + 1, :] = s
         parts.append(jnp.sum(jnp.where(inside, m + jnp.log(s) - t, 0.0), axis=1, keepdims=True))
@@ -398,19 +402,28 @@
         bc_copy(d).start()
         return carry
 
-    def bc_wait_near(d, carry):
-        @pl.when(is_near(lax.rem(chip + chips - d, chips)))
+    first_four = [source(r, 2) for r in range(RINGS)]
+
+    def is_first(c):
+        near = c == first_four[0]
+        for r in range(1, RINGS):
+            near = near | (c == first_four[r])
+        return near
+
+    def bc_wait_first(d, carry):
+        @pl.when(is_first(lax.rem(chip + chips - d, chips)))
         def _():
             bc_copy(d).wait_recv()
         return carry
 
-    def bc_wait_far(d, carry):
-        @pl.when(jnp.logical_not(is_near(lax.rem(chip + chips - d, chips))))
+    def bc_wait_rest(d, carry):
+        @pl.when(jnp.logical_not(is_first(lax.rem(chip + chips - d, chips))))
         def _():
             bc_copy(d).wait_recv()
         bc_copy(d).wait_send()
         lab_copy(d).wait_send()
-        pltpu.make_async_copy(st_out.at[d], st_out.at[d], st_send.at[d]).wait()
+        for r in range(RINGS):
+            run_copy(d - 1, r).wait_send()
         return carry
 
     ls_copy = pltpu.make_async_remote_copy(
@@ -418,33 +431,58 @@
         device_id={"tp": partner}, device_id_type=MESH)
 
     lax.fori_loop(1, chips, bc_start, 0)
-    with jax.named_scope("bc_near"):
-        lax.fori_loop(1, chips, bc_wait_near, 0)
-
-    def form_g(slot, src_stage):
+
+    def e_read(g):
+        return pltpu.make_async_copy(e_hbm.at[lax.rem(g, chips)], stage.at[lax.rem(g, 2)], er_sem.at[lax.rem(g, 2)])
+
+    e_read(1).start()
+    for pair in range(HALF):
+        e_write(chips - 1, pair).wait()
+    e_read(2).start()
+    for mb in range(MBLOCKS):
+        xt_write(chips - 1, mb).wait()
+
+    def xt_read(mb):
+        return pltpu.make_async_copy(
+            xt_hbm.at[pl.ds(pl.multiple_of(mb * mb_rows, mb_rows), mb_rows), :], xtb.at[lax.rem(mb, 2)],
+            xtr_sem.at[lax.rem(mb, 2)])
+
+    xt_read(0).start()
+    for k in range(chips - 5, chips - 1):
+        for j in range(BLOCKS):
+            for r in range(RINGS):
+                ag_copy(k, j, r).wait_send()
+
+    with jax.named_scope("bc_first"):
+        lax.fori_loop(1, chips, bc_wait_first, 0)
+
+    def form_g(g):
+        slot = lax.rem(g, chips)
+        half = lax.rem(g, 2)
         k0 = pl.multiple_of(slot * slot_rows, slot_rows)
         sources = sources_of(slot)
+        holders = sources_of(lax.rem(slot + 1, chips))
         lab = labc.at[0]
         fill_labels(lab, sources)
         for r in range(RINGS):
             rs = slice(r * rt, (r + 1) * rt)
-            m_run[rs, :] = jnp.broadcast_to(to_col(bc_in[sources[r], r:r + 1, :]), (rt, 128))
+            m_run[rs, :] = jnp.broadcast_to(to_col(bc_in[holders[r], r:r + 1, :]), (rt, 128))
             s_run[rs, :] = jnp.broadcast_to(
-                1.0 / (to_col(bc_in[sources[r], RINGS + r:RINGS + r + 1, :]) * tokens), (rt, 128))
+                1.0 / (to_col(bc_in[holders[r], RINGS + r:RINGS + r + 1, :]) * tokens), (rt, 128))
         for lp in range(PIECES):
             off = base(lp)
             for c in range(8):
                 rs = slice(c * chunk, (c + 1) * chunk)
                 rel = lab[rs, :] - off
-                scale = jnp.exp(src_stage[lp, rs, shift] - m_run[rs, :]) * s_run[rs, :]
+                scale = jnp.exp(stage[half, lp, rs, shift] - m_run[rs, :]) * s_run[rs, :]
                 for i, cs in enumerate(cols4):
-                    g = src_stage[lp, rs, cs] * scale - jnp.where(lane_iota + i * 128 == rel, 1.0 / tokens, 0.0)
-                    xg[lp, pl.ds(pl.multiple_of(k0 + c * chunk, chunk), chunk), cs] = g.astype(BF16)
-
-    e_read(1, 1).wait()
+                    v = stage[half, lp, rs, cs] * scale - jnp.where(lane_iota + i * 128 == rel, 1.0 / tokens, 0.0)
+                    xg[lp, pl.ds(pl.multiple_of(k0 + c * chunk, chunk), chunk), cs] = v.astype(BF16)
+
+    e_read(1).wait()
     with jax.named_scope("g_first"):
-        form_g(1, stage1)
-    e_read(3, 1).start()
+        form_g(1)
+    e_read(3).start()
 
     def rs_copy(s, j, r):
         b0, b1 = lax.rem(s, BUFS), lax.rem(s + 1, BUFS)
@@ -455,7 +493,8 @@
 
     def dw_copy(mb, o):
         return pltpu.make_async_remote_copy(
-            src_ref=stage.at[o, :, pl.ds(0, pc)], dst_ref=stage1.at[lax.rem(mb, 2) * HALF + o, :, pl.ds(0, pc)], send_sem=dw_send.at[o],
+            src_ref=stage.at[0, o, :, pl.ds(0, pc)], dst_ref=stage.at[1, lax.rem(mb, 2) * HALF + o, :, pl.ds(0, pc)],
+            send_sem=dw_send.at[o],
             recv_sem=dw_recv.at[lax.rem(mb, 2), o], device_id={"tp": partner}, device_id_type=MESH)
 
     def dw_out(mb, o):
@@ -469,11 +508,9 @@
                 pltpu.make_async_copy(xtb.at[0, pl.ds(rows, rows), cols], dxb.at[:, cols], dxo_sem.at[j, 1]))
 
     last = chips - 1
-    g_iters = chips // 2
-    dw_iters = MBLOCKS * PIECES
-    dw_from = 1 + g_iters
-    own_from = dw_from + dw_iters
-    assert own_from == last * BLOCKS - BLOCKS + 1
+    dw_from = 3 * BLOCKS
+    own_from = last * BLOCKS
+    assert own_from - dw_from == MBLOCKS * PIECES and dw_from - 1 + BLOCKS == chips - 1
 
     def dx_dot(slot, j):
         k0 = pl.multiple_of(slot * slot_rows, slot_rows)
@@ -481,7 +518,7 @@
         for lp in range(PIECES):
             part = lax.dot_general(
                 xg[lp, pl.ds(k0, slot_rows), :],
-                wv[lp // HALF, pl.ds(pl.multiple_of(j * hb, hb), hb), (lp % HALF) * pc:(lp % HALF + 1) * pc],
+                wv[lp, pl.ds(pl.multiple_of(j * hb, hb), hb), :],
                 (((1,), (1,)), ((), ())), preferred_element_type=F32)
             tile = part if tile is None else tile + part
         return tile
@@ -512,28 +549,32 @@
         s = i // BLOCKS
         j = lax.rem(i, BLOCKS)
         b0 = lax.rem(s, BUFS)
+        double = s == 1
+        g = jnp.where(s == 0, i + 1, jnp.where(double, 2 * i - BLOCKS + 1, i + BLOCKS + 1))
 
         @pl.when(s >= 1)
         def _():
             rs_arrive(s, j)
 
-        even = lax.rem(2 * i, chips)
-        e_read(even, 0).wait()
+        e_read(g).wait()
         with jax.named_scope("dx_g"):
             buf[b0, j] = buf[b0, j] + dx_dot(s + 1, j)
-            form_g(even, stage)
+            form_g(g)
         rs_send_on(s, j)
 
-        @pl.when(i < g_iters)
-        def _():
-            e_read(lax.rem(2 * i + 2, chips), 0).start()
-            e_read(2 * i + 1, 1).wait()
+        @pl.when(g + 2 <= chips)
+        def _():
+            e_read(g + 2).start()
+
+        @pl.when(double)
+        def _():
+            e_read(g + 1).wait()
             with jax.named_scope("g"):
-                form_g(2 * i + 1, stage1)
-
-        @pl.when(i < g_iters - 1)
-        def _():
-            e_read(2 * i + 3, 1).start()
+                form_g(g + 1)
+
+            @pl.when(g + 3 <= chips)
+            def _():
+                e_read(g + 3).start()
 
         @pl.when(s >= 1)
         def _():
@@ -544,8 +585,8 @@
         buf[0, 0] = dx_dot(1, 0)
     rs_send_on(0, 0)
     with jax.named_scope("bc_far"):
-        lax.fori_loop(1, chips, bc_wait_far, 0)
-    lax.fori_loop(1, 1 + g_iters, scatter_g, 0)
+        lax.fori_loop(1, chips, bc_wait_rest, 0)
+    lax.fori_loop(1, dw_from, scatter_g, 0)
     pl.semaphore_signal(dw_credit, inc=1, device_id={"tp": partner}, device_id_type=MESH)
     total = bc_in[0]
     for c in range(1, chips):
@@ -576,7 +617,7 @@
 
         with jax.named_scope("dx_dw"):
             buf[b0, j] = buf[b0, j] + dx_dot(s + 1, j)
-            stage[o, :, 0:pc] = jnp.dot(xtb[lax.rem(mb, 2)], xg[lax.rem(o + HALF, PIECES)], preferred_element_type=F32)
+            stage[0, o, :, 0:pc] = jnp.dot(xtb[lax.rem(mb, 2)], xg[lax.rem(o + HALF, PIECES)], preferred_element_type=F32)
         rs_send_on(s, j)
 
         @pl.when((o == 0) & (mb != 1))
@@ -595,7 +636,7 @@
             @pl.when(mb >= 1)
             def _():
                 dw_out(mb - 1, h).wait()
-            dwb[h] = (stage[o, :, 0:pc] + stage1[lax.rem(mb, 2) * HALF + h, :, 0:pc]).astype(BF16)
+            dwb[h] = (stage[0, o, :, 0:pc] + stage[1, lax.rem(mb, 2) * HALF + h, :, 0:pc]).astype(BF16)
             dw_out(mb, h).start()
 
             @pl.when((h == HALF - 1) & (mb < MBLOCKS - 2))
@@ -607,30 +648,13 @@
 
     lax.fori_loop(dw_from, own_from, scatter_dw, 0)
 
-    def scatter_own(i, carry):
-        s = i // BLOCKS
-        j = lax.rem(i, BLOCKS)
-        b0 = lax.rem(s, BUFS)
-        rs_arrive(s, j)
-        with jax.named_scope("dx"):
-            buf[b0, j] = buf[b0, j] + dx_dot(s + 1, j)
-        rs_send_on(s, j)
-
+    def scatter_last(j, carry):
         with jax.named_scope("own"):
-            stage1[j, :, 0:pc] = dx_dot(0, j)
-
-        @pl.when(j == 1)
-        def _():
-            stage1[0, :, 0:pc] = dx_dot(0, 0)
-        rs_release(s, j)
-        return carry
-
-    lax.fori_loop(own_from, last * BLOCKS, scatter_own, 0)
-
-    def scatter_last(j, carry):
+            stage[0, PIECES - 1, :, 0:pc] = dx_dot(0, j)
         rs_arrive(last, j)
         with jax.named_scope("out"):
-            xtb[0, 0:slot_rows, pl.ds(pl.multiple_of(j * hb, hb), hb)] = (buf[last % BUFS, j] + stage1[j, :, 0:pc]).astype(BF16)
+            xtb[0, 0:slot_rows, pl.ds(pl.multiple_of(j * hb, hb), hb)] = (
+                buf[last % BUFS, j] + stage[0, PIECES - 1, :, 0:pc]).astype(BF16)
         for c in dx_out(j):
             c.start()
         rs_release(last, j)
@@ -678,11 +702,9 @@
             in_specs=[any_spec, any_spec, vmem_spec, vmem_spec, any_spec],
             out_specs=(pl.BlockSpec(memory_space=pltpu.SMEM), any_spec, any_spec, any_spec, any_spec, any_spec),
             scratch_shapes=[
-                pltpu.VMEM((2, hidden, shard), BF16),
+                pltpu.VMEM((PIECES, hidden, pc), BF16),
                 pltpu.VMEM((PIECES, all_rows, pc), BF16),
-                pltpu.VMEM((PIECES, slot_rows, pc + 128), F32),
-                pltpu.VMEM((PIECES, slot_rows, pc + 128), F32),
-                pltpu.VMEM((hidden, slot_rows), BF16),
+                pltpu.VMEM((2, PIECES, slot_rows, pc + 128), F32),
                 pltpu.VMEM((2, mb_rows, all_rows), BF16),
                 pltpu.VMEM((BUFS, BLOCKS, slot_rows, hb), F32),
                 pltpu.VMEM((HALF, mb_rows, pc), BF16),

time: 305 us -> 290 us (0.951)
  Pallas kernels: 296 us -> 280 us
    pallas_call x1, Pallas kernels: 296 us -> 280 us  [local_step(): pl.pallas_call(functools.partial(head_kernel, group), name='head', out_sh...]
where the time goes in v1:
time: 290 us; the launch traced here: 289 us
  Pallas kernels  280 us (97%)
  local copies, waits for them, and re-layouts  8.69 us (3%)
    pallas_call x1, Pallas kernels, local_step(): pl.pallas_call(functools.partial(head_kernel, group), name='head', out_sh...  280 us
    unnamed x8, local copies, waits for them, and re-layouts  8.69 us

profile of v1, /device:TPU:97, one launch (start us, length us, event | category | flops | bytes accessed | tf_op | source)
XLA Modules:
  0.0 289.1 jit_solution(6698801406487561895)
XLA Ops:
  0.6 279.8 %head.1 = (f32[2]{0:T(128)}, bf16[2048,1536]{1,0:T(8,128)(2,1)}, bf16[128,2048]{1,0:T(8,128)(2,1)}, bf16[128,2048]{1,0:T(8,128)(2,1)}, f32[16,6,256,640]{3,2,1,0:T(8,128)}, /*index=5*/bf16[2048,4096]{1,0:T(8,128)(2,1)}) custom-call(bf16[128,2048]{1,0:T(8,128)(2,1)} %refs_0_.1, bf16[128,2048]{1,0:T(8,128)(2,1)} %refs_1_.1, s32[1,128]{1,0:T(1,128)} %bitcast.2, ...), custom_call_target="tpu_custom_call" | custom-call | tf_op jit(solution)/shard_map/head/pallas_call | solution.py:691
  280.4 1.1 copy.13
  281.6 0.0 copy-start.1
  281.6 0.0 copy-start
  281.6 6.0 %copy.14 = bf16[2048,1536]{1,0:T(8,128)(2,1)} copy(bf16[2048,1536]{1,0:T(8,128)(2,1)} %get-tuple-element.17) | data formatting | bytes 12582912
  287.5 0.0 copy-done.1
  287.5 0.8 copy.15
  288.3 0.0 copy-done
  288.3 0.8 copy.16
Async XLA Ops:
  281.6 6.0 %copy-start.1 = (bf16[128,2048]{1,0:T(8,128)(2,1)S(1)}, bf16[128,2048]{1,0:T(8,128)(2,1)}, u32[]{:S(2)}) copy-start(bf16[128,2048]{1,0:T(8,128)(2,1)} %get-tuple-element.18) | copy-start | bytes 1572868
  281.6 6.8 %copy-start = (bf16[128,2048]{1,0:T(8,128)(2,1)S(1)}, bf16[128,2048]{1,0:T(8,128)(2,1)}, u32[]{:S(2)}) copy-start(bf16[128,2048]{1,0:T(8,128)(2,1)} %get-tuple-element.19) | copy-start | bytes 1572868

commit v2 on v1

--- a/solution.py
+++ b/solution.py
@@ -19,6 +19,19 @@
 BUFS = 3
 
 
+class Both:
+    def __init__(self, *copies):
+        self.copies = copies
+
+    def start(self):
+        for c in self.copies:
+            c.start()
+
+    def wait(self):
+        for c in self.copies:
+            c.wait()
+
+
 def head_kernel(group, *refs):
     chips = group // 2
     dma = pltpu.SemaphoreType.DMA
@@ -27,15 +40,15 @@
         functools.partial(head_body, group, *refs),
         x_sem=dma((2 * BLOCKS,)), w_sem=dma((HALF,)), wp_sem=dma((2, HALF)), lab_sem=dma((2, chips)), sync=regular((3,)),
         ag_send=dma((4, BLOCKS * RINGS)), ag_recv=dma((chips, BLOCKS * RINGS)),
-        e_sem=dma((HALF,)), er_sem=dma((2,)), xt_sem=dma((MBLOCKS,)), xtr_sem=dma((2,)),
+        e_sem=dma((2, HALF)), er_sem=dma((2, 2)), xt_sem=dma((MBLOCKS,)), xtr_sem=dma((2,)),
         run_send=dma((chips, RINGS)), run_recv=dma((chips, RINGS)), bc_send=dma((chips,)), bc_recv=dma((chips,)),
         ls_sem=dma((2,)), rs_send=dma((BUFS, BLOCKS, RINGS)), rs_recv=dma((BUFS, BLOCKS, RINGS)),
         credit=regular((BLOCKS, RINGS)), dw_send=dma((HALF,)), dw_recv=dma((2, HALF)), dw_credit=regular,
         dwo_sem=dma((HALF,)), dxo_sem=dma((BLOCKS, 2)))
 
 
-def head_body(group, xa, xb, la, lb, w, loss, dw, dxa, dxb, e_hbm, xt_hbm,
-              wv, xg, stage, xtb, buf, dwb, m_run, s_run, t_run, labc,
+def head_body(group, xa, xb, la, lb, w, loss, dw, dxa, dxb, e_hbm, m_hbm, xt_hbm,
+              wv, xg, stage, shift, xtb, buf, dwb, m_run, s_run, t_run, labc,
               lab_in, run_out, run_in, bc_in, bc_out, ls_out, ls_in,
               x_sem, w_sem, wp_sem, lab_sem, sync, ag_send, ag_recv, e_sem, er_sem, xt_sem, xtr_sem, run_send, run_recv,
               bc_send, bc_recv, ls_sem, rs_send, rs_recv, credit, dw_send, dw_recv, dw_credit, dwo_sem, dxo_sem):
@@ -195,31 +208,33 @@
         return owner * shard + (lp % HALF) * pc
 
     chunk = slot_rows // 8
-    lane_iota = lax.broadcasted_iota(jnp.int32, (chunk, 128), 1)
-    cols4 = [slice(c * 128, (c + 1) * 128) for c in range(pc // 128)]
-    shift = slice(pc, pc + 128)
+    per = pc // 128
+    lane_at = [lax.broadcasted_iota(jnp.int32, (chunk, 128), 1) + i * 128 for i in range(per)]
+    vregs = [(i // per, i % per, slice(i % per * 128, (i % per + 1) * 128)) for i in range(2 * per)]
+
+    def hits(lab_rows, pair):
+        rel = [lab_rows - base(2 * pair), lab_rows - base(2 * pair + 1)]
+        return [lane_at[n] == rel[h] for h, n, _ in vregs]
 
     def z_dot(k0, lp):
         z = None
         for b in range(BLOCKS):
             part = jnp.dot(xg[b, pl.ds(k0, slot_rows), :], wv[lp, b * hb:(b + 1) * hb, :], preferred_element_type=F32)
             z = part if z is None else z + part
-        stage[0, lp, :, 0:pc] = z
-
-    def z_stats(lp, lab):
-        off = base(lp)
+        stage[0, lp // 2, lp % 2] = z
+
+    def z_stats(pair, lab):
         for c in range(8):
             rs = slice(c * chunk, (c + 1) * chunk)
-            z = [stage[0, lp, rs, cs] for cs in cols4]
+            z = [stage[0, pair, h, rs, cs] for h, _, cs in vregs]
             m = functools.reduce(jnp.maximum, z)
             e = [jnp.exp(v - m) for v in z]
-            rel = lab[rs, :] - off
-            t = functools.reduce(jnp.add, [jnp.where(lane_iota + i * 128 == rel, v, 0.0) for i, v in enumerate(z)])
+            t = functools.reduce(jnp.add, [jnp.where(h, v, 0.0) for h, v in zip(hits(lab[rs, :], pair), z)])
             s = functools.reduce(jnp.add, e)
-            for cs, v in zip(cols4, e):
-                stage[0, lp, rs, cs] = v
-            stage[0, lp, rs, shift] = m
-            if lp == 0:
+            for (h, _, cs), v in zip(vregs, e):
+                stage[0, pair, h, rs, cs] = v
+            shift[0, pair, rs, :] = m
+            if pair == 0:
                 m_run[rs, :] = m
                 s_run[rs, :] = s
                 t_run[rs, :] = t
@@ -231,8 +246,8 @@
                 t_run[rs, :] = t_run[rs, :] + t
 
     def e_write(slot, pair):
-        two = pl.ds(2 * pair, 2)
-        return pltpu.make_async_copy(stage.at[0, two], e_hbm.at[slot, two], e_sem.at[pair])
+        return Both(pltpu.make_async_copy(stage.at[0, pair], e_hbm.at[slot, pair], e_sem.at[0, pair]),
+                    pltpu.make_async_copy(shift.at[0, pair], m_hbm.at[slot, pair], e_sem.at[1, pair]))
 
     def xt_write(slot, mb):
         return pltpu.make_async_copy(
@@ -300,13 +315,23 @@
         with jax.named_scope("u0"):
             z_dot(k0, 0)
             z_dot(k0, 1)
-            z_stats(4, other)
-            z_stats(5, other)
+            z_stats(2, other)
 
         @pl.when(slot == 0)
         def _():
             poll(k, 0)
-        poll(k, 1)
+
+        @pl.when(k == 2)
+        def _():
+            poll(k, 3)
+
+        @pl.when(k == 3)
+        def _():
+            poll(k, 2)
+
+        @pl.when((k < 2) | (k > 3))
+        def _():
+            poll(k, 1)
 
         @pl.when(slot >= 1)
         def _():
@@ -326,9 +351,19 @@
             z_dot(k0, 2)
             z_dot(k0, 3)
             z_stats(0, here)
-            z_stats(1, here)
         e_write(slot, 0).start()
-        poll(k, 2)
+
+        @pl.when(k == 2)
+        def _():
+            poll(k + 1, 0)
+
+        @pl.when(k == 3)
+        def _():
+            poll(k, 3)
+
+        @pl.when((k < 2) | (k > 3))
+        def _():
+            poll(k, 2)
 
         @pl.when(slot == 0)
         def _():
@@ -337,6 +372,7 @@
             lab_wait(True)
             poll(k, 3)
             poll(k + 1, 0)
+            poll(k + 1, 1)
             w_swap(1).wait()
             w_swap(2).wait()
 
@@ -353,8 +389,7 @@
         with jax.named_scope("u2"):
             z_dot(k0, 4)
             z_dot(k0, 5)
-            z_stats(2, here)
-            z_stats(3, here)
+            z_stats(1, here)
             fill_labels(other, ahead)
             for mb in range(MBLOCKS):
                 at = mb * mb_rows % hb
@@ -363,7 +398,12 @@
         for mb in range(MBLOCKS):
             xt_write(slot, mb).start()
 
-        @pl.when(slot >= 1)
+        for early in range(1, 4):
+            @pl.when(k == early)
+            def _():
+                poll(k + 1, 3 - early)
+
+        @pl.when(k >= 4)
         def _():
             poll(k, 3)
             poll(k + 1, 0)
@@ -376,8 +416,7 @@
 
     lax.fori_loop(1, chips + 1, gather_step, 0)
     with jax.named_scope("flush"):
-        z_stats(4, labc.at[(chips - 1) % 2])
-        z_stats(5, labc.at[(chips - 1) % 2])
+        z_stats(2, labc.at[(chips - 1) % 2])
     e_write(chips - 1, 2).start()
     join_stats(chips - 1)
 
@@ -433,7 +472,9 @@
     lax.fori_loop(1, chips, bc_start, 0)
 
     def e_read(g):
-        return pltpu.make_async_copy(e_hbm.at[lax.rem(g, chips)], stage.at[lax.rem(g, 2)], er_sem.at[lax.rem(g, 2)])
+        slot, half = lax.rem(g, chips), lax.rem(g, 2)
+        return Both(pltpu.make_async_copy(e_hbm.at[slot], stage.at[half], er_sem.at[0, half]),
+                    pltpu.make_async_copy(m_hbm.at[slot], shift.at[half], er_sem.at[1, half]))
 
     e_read(1).start()
     for pair in range(HALF):
@@ -469,15 +510,14 @@
             m_run[rs, :] = jnp.broadcast_to(to_col(bc_in[holders[r], r:r + 1, :]), (rt, 128))
             s_run[rs, :] = jnp.broadcast_to(
                 1.0 / (to_col(bc_in[holders[r], RINGS + r:RINGS + r + 1, :]) * tokens), (rt, 128))
-        for lp in range(PIECES):
-            off = base(lp)
+        for pair in range(HALF):
             for c in range(8):
                 rs = slice(c * chunk, (c + 1) * chunk)
-                rel = lab[rs, :] - off
-                scale = jnp.exp(stage[half, lp, rs, shift] - m_run[rs, :]) * s_run[rs, :]
-                for i, cs in enumerate(cols4):
-                    v = stage[half, lp, rs, cs] * scale - jnp.where(lane_iota + i * 128 == rel, 1.0 / tokens, 0.0)
-                    xg[lp, pl.ds(pl.multiple_of(k0 + c * chunk, chunk), chunk), cs] = v.astype(BF16)
+                krs = pl.ds(pl.multiple_of(k0 + c * chunk, chunk), chunk)
+                scale = jnp.exp(shift[half, pair, rs, :] - m_run[rs, :]) * s_run[rs, :]
+                for (h, _, cs), hit in zip(vregs, hits(lab[rs, :], pair)):
+                    v = stage[half, pair, h, rs, cs] * scale - jnp.where(hit, 1.0 / tokens, 0.0)
+                    xg[2 * pair + h, krs, cs] = v.astype(BF16)
 
     e_read(1).wait()
     with jax.named_scope("g_first"):
@@ -491,9 +531,12 @@
             send_sem=rs_send.at[b0, j, r], recv_sem=rs_recv.at[b1, j, r],
             device_id=dev(down[r]), device_id_type=MESH)
 
+    def tile_at(h, o):
+        return (h, o // 2, lax.rem(o, 2))
+
     def dw_copy(mb, o):
         return pltpu.make_async_remote_copy(
-            src_ref=stage.at[0, o, :, pl.ds(0, pc)], dst_ref=stage.at[1, lax.rem(mb, 2) * HALF + o, :, pl.ds(0, pc)],
+            src_ref=stage.at[tile_at(0, o)], dst_ref=stage.at[tile_at(1, lax.rem(mb, 2) * HALF + o)],
             send_sem=dw_send.at[o],
             recv_sem=dw_recv.at[lax.rem(mb, 2), o], device_id={"tp": partner}, device_id_type=MESH)
 
@@ -617,7 +660,7 @@
 
         with jax.named_scope("dx_dw"):
             buf[b0, j] = buf[b0, j] + dx_dot(s + 1, j)
-            stage[0, o, :, 0:pc] = jnp.dot(xtb[lax.rem(mb, 2)], xg[lax.rem(o + HALF, PIECES)], preferred_element_type=F32)
+            stage[tile_at(0, o)] = jnp.dot(xtb[lax.rem(mb, 2)], xg[lax.rem(o + HALF, PIECES)], preferred_element_type=F32)
         rs_send_on(s, j)
 
         @pl.when((o == 0) & (mb != 1))
@@ -636,7 +679,7 @@
             @pl.when(mb >= 1)
             def _():
                 dw_out(mb - 1, h).wait()
-            dwb[h] = (stage[0, o, :, 0:pc] + stage[1, lax.rem(mb, 2) * HALF + h, :, 0:pc]).astype(BF16)
+            dwb[h] = (stage[tile_at(0, o)] + stage[tile_at(1, lax.rem(mb, 2) * HALF + h)]).astype(BF16)
             dw_out(mb, h).start()
 
             @pl.when((h == HALF - 1) & (mb < MBLOCKS - 2))
@@ -650,11 +693,11 @@
 
     def scatter_last(j, carry):
         with jax.named_scope("own"):
-            stage[0, PIECES - 1, :, 0:pc] = dx_dot(0, j)
+            stage[0, HALF - 1, 1] = dx_dot(0, j)
         rs_arrive(last, j)
         with jax.named_scope("out"):
             xtb[0, 0:slot_rows, pl.ds(pl.multiple_of(j * hb, hb), hb)] = (
-                buf[last % BUFS, j] + stage[0, PIECES - 1, :, 0:pc]).astype(BF16)
+                buf[last % BUFS, j] + stage[0, HALF - 1, 1]).astype(BF16)
         for c in dx_out(j):
             c.start()
         rs_release(last, j)
@@ -672,6 +715,26 @@
     for j in range(BLOCKS):
         for c in dx_out(j):
             c.wait()
+
+
+def copy_kernel(loss, dw, dxa, dxb, loss_out, dw_out, dxa_out, dxb_out, dw_v, dxa_v, dxb_v, in_sem, out_sem):
+    moves = []
+    for n, (src, via, dst) in enumerate(((dw, dw_v, dw_out), (dxa, dxa_v, dxa_out), (dxb, dxb_v, dxb_out))):
+        parts = MBLOCKS if n == 0 else 1
+        size = src.shape[0] // parts
+        for p in range(parts):
+            at = pl.ds(p * size, size)
+            moves.append((pltpu.make_async_copy(src.at[at], via.at[at], in_sem.at[n, p]),
+                          pltpu.make_async_copy(via.at[at], dst.at[at], out_sem.at[n, p])))
+    for load, _ in moves:
+        load.start()
+    loss_out[0] = loss[0]
+    loss_out[1] = loss[1]
+    for load, store in moves:
+        load.wait()
+        store.start()
+    for _, store in moves:
+        store.wait()
 
 
 def solution(mesh):
@@ -696,15 +759,17 @@
                 jax.ShapeDtypeStruct((hidden, shard), BF16),
                 jax.ShapeDtypeStruct((rows, hidden), BF16),
                 jax.ShapeDtypeStruct((rows, hidden), BF16),
-                jax.ShapeDtypeStruct((chips, PIECES, slot_rows, pc + 128), F32),
+                jax.ShapeDtypeStruct((chips, HALF, 2, slot_rows, pc), F32),
+                jax.ShapeDtypeStruct((chips, HALF, slot_rows, 128), F32),
                 jax.ShapeDtypeStruct((hidden, all_rows), BF16),
             ),
             in_specs=[any_spec, any_spec, vmem_spec, vmem_spec, any_spec],
-            out_specs=(pl.BlockSpec(memory_space=pltpu.SMEM), any_spec, any_spec, any_spec, any_spec, any_spec),
+            out_specs=(pl.BlockSpec(memory_space=pltpu.SMEM),) + (any_spec,) * 6,
             scratch_shapes=[
                 pltpu.VMEM((PIECES, hidden, pc), BF16),
                 pltpu.VMEM((PIECES, all_rows, pc), BF16),
-                pltpu.VMEM((2, PIECES, slot_rows, pc + 128), F32),
+                pltpu.VMEM((2, HALF, 2, slot_rows, pc), F32),
+                pltpu.VMEM((2, HALF, slot_rows, 128), F32),
                 pltpu.VMEM((2, mb_rows, all_rows), BF16),
                 pltpu.VMEM((BUFS, BLOCKS, slot_rows, hb), F32),
                 pltpu.VMEM((HALF, mb_rows, pc), BF16),
@@ -712,9 +777,9 @@
                 pltpu.VMEM((slot_rows, 128), F32),
                 pltpu.VMEM((slot_rows, 128), F32),
                 pltpu.VMEM((2, slot_rows, 128), jnp.int32),
-                pltpu.VMEM((chips, 8, rows), F32),
-                pltpu.VMEM((chips, RINGS, 8, 128), F32),
-                pltpu.VMEM((chips, RINGS, 8, 128), F32),
+                pltpu.VMEM((chips, 2, rows), F32),
+                pltpu.VMEM((chips, RINGS, 4, 128), F32),
+                pltpu.VMEM((chips, RINGS, 4, 128), F32),
                 pltpu.VMEM((chips, 8, 128), F32),
                 pltpu.VMEM((8, 128), F32),
                 pltpu.VMEM((8, 128), F32),
@@ -723,7 +788,16 @@
             compiler_params=pltpu.CompilerParams(
                 collective_id=0, has_side_effects=True, vmem_limit_bytes=67043328),
         )(x_a, x_b, labels_a.reshape(1, rows), labels_b.reshape(1, rows), w_local)
-        return out[0], out[1], out[2], out[3]
+        results = out[:4]
+        return pl.pallas_call(
+            copy_kernel,
+            name="results",
+            out_shape=tuple(jax.ShapeDtypeStruct(v.shape, v.dtype) for v in results),
+            in_specs=[pl.BlockSpec(memory_space=pltpu.SMEM), any_spec, any_spec, any_spec],
+            out_specs=(pl.BlockSpec(memory_space=pltpu.SMEM), any_spec, any_spec, any_spec),
+            scratch_shapes=[pltpu.VMEM(v.shape, v.dtype) for v in results[1:]] + [
+                pltpu.SemaphoreType.DMA((3, MBLOCKS)), pltpu.SemaphoreType.DMA((3, MBLOCKS))],
+        )(*results)
 
     row_spec = P(("dp", "tp"), None)
     label_spec = P(("dp", "tp"))

time: 290 us -> 288 us (level)
  local copies, waits for them, and re-layouts: 8.69 us -> 0 us
  Pallas kernels: 280 us -> 286 us
    unnamed x8 -> x0, local copies, waits for them, and re-layouts: 8.69 us -> none
    pallas_call x0 -> x1, Pallas kernels: none -> 7.3 us  [local_step(): pl.pallas_call(copy_kernel, name='results', out_shape=tuple((jax.ShapeDty...]
where the time goes in v2:
time: 288 us; the launch traced here: 287 us
  Pallas kernels  286 us (99%)
    pallas_call x1, Pallas kernels, local_step(): pl.pallas_call(functools.partial(head_kernel, group), name='head', out_sh...  279 us
    pallas_call x1, Pallas kernels, local_step(): pl.pallas_call(copy_kernel, name='results', out_shape=tuple((jax.ShapeDty...  7.3 us

profile of v2, /device:TPU:97, one launch (start us, length us, event | category | flops | bytes accessed | tf_op | source)
XLA Modules:
  0.0 286.8 jit_solution(16998002627536489054)
XLA Ops:
  0.6 278.8 %head.1 = (f32[2]{0:T(128)}, bf16[2048,1536]{1,0:T(8,128)(2,1)}, bf16[128,2048]{1,0:T(8,128)(2,1)}, bf16[128,2048]{1,0:T(8,128)(2,1)}, f32[16,3,2,256,512]{4,3,2...) custom-call(bf16[128,2048]{1,0:T(8,128)(2,1)} %refs_0_.1, bf16[128,2048]{1,0:T(8,128)(2,1)} %refs_1_.1, ...), custom_call_target="tpu_custom_call" | custom-call | tf_op jit(solution)/shard_map/head/pallas_call | solution.py:754
  279.5 7.3 %results.1 = (f32[2]{0:T(128)}, bf16[2048,1536]{1,0:T(8,128)(2,1)}, bf16[128,2048]{1,0:T(8,128)(2,1)}, bf16[128,2048]{1,0:T(8,128)(2,1)}) custom-call(f32[2]{0:T(128)} %get-tuple-element.8.loss, bf16[2048,1536]{1,0:T(8,128)(2,1)} %get-tuple-element.9.dw, bf16[128,2048]{1,0:T(8,128)(2,1)} %get-tuple-element.10.dxa, bf16[128,2048]{1,0:T(8,128)(2,1)} %get-tuple-element.11.dxb), custom_call_target="tpu_custom_call" | custom-call | tf_op jit(solution)/shard_map/results/pallas_call | solution.py:792
